TPU v7x, 32 devices: a whole 2x2x4 slice. The times are simulated.
32 devices in a mesh: grp: 8 (over z, y), slab: 4 (over x, core).
Axes of the slice: x: 2, y: 2, z: 4, core: 2. Of those that a mesh axis runs over, the one named last changes fastest.
Arguments:
- grids: float32 [8, 512, 4096], P('grp', 'slab'), may hold values from -6 to 6
- first_level: int32 [8], P('grp'), may hold values from 6 to 8, as said below
- coeffs: int32 [8], P('grp'), may hold values from -3 to 3
- slot_map: int32 [8, 512], P('grp', 'slab'), may hold values from 0 to 1023, as said below
Outputs:
- combined_grid: float32 [8, 512, 4096], P('grp', 'slab')
Inputs may be any that keep to these rules, and one draw needn't show every extreme that they name: The second dimension of grid g has level 9 minus first_level[g]. Every value of the range is taken by some grid. `slot_map`: grid g's point with first coordinate i of 2^a points lies at position i / 2^a of a periodic unit interval, and likewise in the second dimension. Two rows of any grids at the same position in the first two dimensions share a slot; rows of one grid have distinct slots; every slot is used by some grid. The rows held by the s-th index of slab (first coordinates in the s-th of 4 equal ranges) of every grid have slots in the s-th of 4 equal aligned ranges of the 1024 slots.
All inputs are finite; a program needn't handle non-finite values.
Results may differ from a plain program's by a relative error of at most 0.0003.
Values sent between devices are 32-bit elements; how exact they have to be, the bound alone decides.
A program may use at most 64 MiB of HBM per device.

v0:
```python
import jax
import jax.numpy as jnp
from jax import lax
from jax.sharding import PartitionSpec as P

P2 = 16
P3 = 16
P4 = 16
LEVEL_SUM = 9
PLANE = 8
ROWS = 512


def hier_weight(target, source, period):
    spread = target & -target
    interior = (target != 0).astype(jnp.float32)
    left_side = (source == target - spread).astype(jnp.float32)
    right_side = (source == (target + spread) % period).astype(jnp.float32)
    return (target == source).astype(jnp.float32) - 0.5 * interior * (left_side + right_side)


def dehier_weight(target, source, period):
    spread = jnp.maximum(source & -source, 1).astype(jnp.float32)
    apart = jnp.abs(target - source)
    apart = jnp.minimum(apart, period - apart).astype(jnp.float32)
    return jnp.where(source == 0, 1.0, jnp.maximum(0.0, 1.0 - apart / spread))


def square_table(maker, length):
    points = jnp.arange(length, dtype=jnp.int32)
    return maker(points[:, None], points[None, :], length)


def inner_apply(values, third_op, rest_op):
    count = values.shape[0]
    shaped = values.reshape(count, P2, P3 * P4)
    shaped = jnp.einsum("ij,rjk->rik", third_op, shaped, precision=lax.Precision.HIGHEST)
    shaped = jnp.einsum("rjk,lk->rjl", shaped, rest_op, precision=lax.Precision.HIGHEST)
    return shaped.reshape(count, P2 * P3 * P4)


def exact_dot(left, right):
    return jnp.dot(left, right, precision=lax.Precision.HIGHEST, preferred_element_type=jnp.float32)


def shards(grids, first_level, coeffs, slot_map):
    grid_rows = grids[0]
    level = first_level[0]
    second = LEVEL_SUM - level
    rows_dev = grid_rows.shape[0]
    width = grid_rows.shape[1]
    slabs = lax.axis_size("slab")
    slab_index = lax.axis_index("slab")
    span = rows_dev >> second
    row_ids = jnp.arange(rows_dev, dtype=jnp.int32)
    first_pos = row_ids >> second
    second_pos = row_ids & (1 << second) - 1
    slab_ids = jnp.arange(slabs, dtype=jnp.int32)
    same_first = (first_pos[:, None] == first_pos[None, :]).astype(jnp.float32)
    hier_third = square_table(hier_weight, P2)
    hier_rest = jnp.kron(square_table(hier_weight, P3), square_table(hier_weight, P4))
    values = inner_apply(grid_rows, hier_third, hier_rest)
    second_op = same_first * hier_weight(second_pos[:, None], second_pos[None, :], 1 << second)
    values = exact_dot(second_op, values)
    plane = values[:PLANE]
    planes = lax.all_gather(plane[None], "slab", axis=0, tiled=True)
    following = lax.dynamic_index_in_dim(planes, (slab_index + 1) % slabs, 0, keepdims=False)
    extended = jnp.concatenate([values, following], axis=0)
    ext_ids = jnp.arange(rows_dev + PLANE, dtype=jnp.int32)
    ext_first = ext_ids >> second
    ext_second = ext_ids & (1 << second) - 1
    spread = first_pos & -first_pos
    interior = (first_pos != 0).astype(jnp.float32)[:, None]
    same_second = (second_pos[:, None] == ext_second[None, :]).astype(jnp.float32)
    centre = (ext_first[None, :] == first_pos[:, None]).astype(jnp.float32)
    below = (ext_first[None, :] == (first_pos - spread)[:, None]).astype(jnp.float32)
    above = (ext_first[None, :] == (first_pos + spread)[:, None]).astype(jnp.float32)
    fine_op = same_second * (centre - 0.5 * interior * (below + above))
    surplus = exact_dot(fine_op, extended)
    coarse_weights = hier_weight(slab_index, slab_ids, slabs)
    coarse = jnp.einsum("q,qpk->pk", coarse_weights, planes, precision=lax.Precision.HIGHEST)
    padded = jnp.concatenate([coarse, jnp.zeros((rows_dev - PLANE, width), jnp.float32)], axis=0)
    surplus = jnp.where((first_pos == 0)[:, None], padded, surplus)
    scaled = coeffs[0].astype(jnp.float32) * surplus
    per_slab = 2 * ROWS // slabs
    slot_local = slot_map[0] % per_slab
    slot_ids = jnp.arange(per_slab, dtype=jnp.int32)
    gather_op = (slot_local[None, :] == slot_ids[:, None]).astype(jnp.float32)
    term = exact_dot(gather_op, scaled)
    total = lax.psum(term, "grp")
    spread_op = (slot_local[:, None] == slot_ids[None, :]).astype(jnp.float32)
    combined = exact_dot(spread_op, total)
    back_third = square_table(dehier_weight, P2)
    back_rest = jnp.kron(square_table(dehier_weight, P3), square_table(dehier_weight, P4))
    values = inner_apply(combined, back_third, back_rest)
    back_second = same_first * dehier_weight(second_pos[:, None], second_pos[None, :], 1 << second)
    values = exact_dot(back_second, values)
    top_plane = values[:PLANE]
    top_planes = lax.all_gather(top_plane[None], "slab", axis=0, tiled=True)
    here_weights = dehier_weight(slab_index, slab_ids, slabs)
    there_weights = dehier_weight((slab_index + 1) % slabs, slab_ids, slabs)
    here = jnp.einsum("q,qpk->pk", here_weights, top_planes, precision=lax.Precision.HIGHEST)
    there = jnp.einsum("q,qpk->pk", there_weights, top_planes, precision=lax.Precision.HIGHEST)
    same_row_second = (second_pos[:, None] == second_pos[None, :]).astype(jnp.float32)
    inside = (first_pos[None, :] != 0).astype(jnp.float32)
    local_op = (
        same_row_second * inside * dehier_weight(first_pos[:, None], first_pos[None, :], 2 * span)
    )
    fraction = first_pos.astype(jnp.float32) / span.astype(jnp.float32)
    plane_ids = jnp.arange(PLANE, dtype=jnp.int32)
    plane_pick = (second_pos[:, None] == plane_ids[None, :]).astype(jnp.float32)
    nodal = exact_dot(local_op, values)
    nodal = nodal + exact_dot((1.0 - fraction)[:, None] * plane_pick, here)
    nodal = nodal + exact_dot(fraction[:, None] * plane_pick, there)
    return nodal[None]


def solution(mesh):
    in_specs = (P("grp", "slab", None), P("grp"), P("grp"), P("grp", "slab"))
    out_specs = P("grp", "slab", None)
    return jax.shard_map(shards, mesh=mesh, in_specs=in_specs, out_specs=out_specs, check_vma=False)
```

profile of v0, /device:TPU:0, one launch (start us, length us, event | category | flops | bytes accessed | tf_op | source)
XLA Modules:
  0.0 230.8 jit_solution(8167477807761341772)
XLA Ops:
  6.5 0.0 all-reduce.3.cloned.1.call-start
  7.3 0.1 and_select_fusion.1
  7.5 2.3 copy.16
  9.7 0.1 multiply_subtract_fusion
  9.8 1.9 fusion.114
  11.8 1.5 broadcast_multiply_fusion.1
  13.3 2.4 %reshape.448 = f32[256,256,1]{1,0,2:T(8,128)S(1)} reshape(f32[16,16,16,16]{3,2,1,0:T(8,128)} %broadcast_multiply_fusion.1) | data formatting | bytes 524288 | tf_op jit(solution)/shard_map/jit(kron)/mul | solution.py:61
  15.7 3.2 %fusion.7 = f32[128,16,256]{0,2,1:T(8,128)S(1)} fusion(f32[256,256,1]{1,0,2:T(8,128)S(1)} %reshape.448, f32[16,128,256]{2,0,1:T(8,128)S(1)} %fusion.114), kind=kOutput, calls=%fused_computation.10 | convolution fusion | flops 1610612736 | bytes 4456448 | tf_op jit(solution)/shard_map/rjk,lk->rjl/dot_general | solution.py:38
  19.0 2.0 fusion.39
  21.0 0.0 copy-start
  21.0 8.8 %all-gather = f32[32,4096]{1,0:T(8,128)S(1)} all-gather(f32[8,4096]{1,0:T(8,128)S(1)} %slice.8), channel_id=2, replica_groups=mesh['grp'=8,'slab'=4] {'slab'}, dimensions={0}, use_global_device_ids=true | all-gather | bytes 655360 | tf_op jit(solution)/shard_map/all_gather | solution.py:66
  29.8 1.2 fusion.11
  31.1 0.1 copy.41
  31.8 0.0 copy-done
  31.8 2.1 fusion.1
  33.9 3.9 %fusion.29 = f32[256,4096]{1,0:T(8,128)} fusion(f32[128,4096]{1,0:T(8,128)S(1)} %fusion.1, s32[128]{0:T(128)S(1)} %fusion.130), kind=kOutput, calls=%fused_computation.38 | convolution fusion | flops 1610645504 | bytes 6291968 | tf_op jit(solution)/shard_map/dot_general | solution.py:43
  37.8 0.0 all-reduce.3.cloned.1.call-update
  37.9 0.2 broadcast_multiply_fusion
  38.1 0.9 reshape.452
  39.1 156.1 %all-reduce.3.cloned.1.call-done = f32[256,4096]{1,0:T(8,128)} async-done(((f32[256,4096]{1,0:T(8,128)}), f32[256,4096]{1,0:T(8,128)}) %all-reduce.3.cloned.1.call-update) | async-done | bytes 4194320 | tf_op jit(solution)/shard_map/psum | solution.py:90
  195.2 3.9 %fusion.28 = f32[128,4096]{1,0:T(8,128)S(1)} fusion(f32[256,4096]{1,0:T(8,128)} %all-reduce.3.cloned.1.call-done, s32[128]{0:T(128)S(1)} %and_select_fusion.3), kind=kOutput, calls=%fused_computation.37 | convolution fusion | flops 1610645504 | bytes 6291968 | tf_op jit(solution)/shard_map/dot_general | solution.py:43
  199.1 0.7 copy.17
  199.8 1.9 fusion.112
  201.7 3.5 %fusion.5 = f32[128,16,256]{0,2,1:T(8,128)S(1)} fusion(f32[256,256,1]{1,0,2:T(8,128)S(1)} %reshape.452, f32[128,256,16]{1,2,0:T(8,128)S(1)} %fusion.112), kind=kOutput, calls=%fused_computation.8 | convolution fusion | flops 1610612736 | bytes 4456448 | tf_op jit(solution)/shard_map/rjk,lk->rjl/dot_general | solution.py:38
  205.2 2.0 fusion.38
  207.2 7.1 %all-gather.1 = f32[32,4096]{1,0:T(8,128)S(1)} all-gather(f32[8,4096]{1,0:T(8,128)S(1)} %slice.9), channel_id=3, replica_groups=mesh['grp'=8,'slab'=4] {'slab'}, dimensions={0}, use_global_device_ids=true | all-gather | bytes 655360 | tf_op jit(solution)/shard_map/all_gather | solution.py:99
  214.4 1.3 fusion.15
  215.6 1.3 fusion.13
  216.9 2.0 fusion.35
  218.9 1.9 convolution_add_fusion.1
  220.8 3.2 %fusion = f32[1,128,4096]{2,1,0:T(8,128)} fusion(f32[128,4096]{1,0:T(8,128)S(1)} %convolution_add_fusion.1, f32[1,8,4096]{2,0,1:T(1,128)S(1)} %fusion.13, f32[128]{0:T(128)S(1)} %get-tuple-element.6, s32[128]{0:T(128)S(1)} %get-tuple-element.13), kind=kOutput, calls=%fused_computation.1 | convolution fusion | flops 50857984 | bytes 4326400 | tf_op jit(solution)/shard_map/dot_general | solution.py:43
  (21 shorter events, 0.2 us)
Async XLA Ops:
  6.5 188.7 %all-reduce.3.cloned.1.call-start = ((), (), s32[]{:S(2)}) async-start(), calls=%async_computation | async-start | bytes 8388608 | tf_op jit(solution)/shard_map/psum | solution.py:90
  21.0 10.9 %copy-start = (s32[1,128]{1,0:T(1,128)S(1)}, s32[1,128]{1,0:T(1,128)}, u32[]{:S(2)}) copy-start(s32[1,128]{1,0:T(1,128)} %param.7) | copy-start | bytes 1540
Sparse Core Ops, SparseCore 0:
  37.9 157.2 all-reduce.2
where the time goes:
time: 231 us
  waiting for transfers between devices  156 us (68%)
  matrix products  35.2 us (15%)
  blocking collectives  16 us (7%)
  between operations  15 us (6%)
  local copies, waits for them, and re-layouts  6.43 us (3%)
    psum x1, waiting for transfers between devices, shards(): total = lax.psum(term, 'grp')  156 us
    dot_general x8, matrix products, exact_dot(): jnp.dot(left, right, precision=lax.Precision.HIGHEST, preferred_element_t...  20.9 us
    all_gather x1, blocking collectives, shards(): planes = lax.all_gather(plane[None], 'slab', axis=0, tiled=True)  8.82 us
    all_gather x1, blocking collectives, shards(): top_planes = lax.all_gather(top_plane[None], 'slab', axis=0, tiled=True)  7.14 us
    dot_general x2, matrix products, inner_apply(): jnp.einsum('rjk,lk->rjl', shaped, rest_op, precision=lax.Precision.HIGHEST)  6.7 us
  transfers between devices with their start and end apart: 1, of which 1 were waited for; matrix products, arithmetic and copies ran while one was open for 1% of the time, Pallas kernels for 0%

commit v1 on v0

--- a/solution.py
+++ b/solution.py
@@ -87,7 +87,10 @@
     slot_ids = jnp.arange(per_slab, dtype=jnp.int32)
     gather_op = (slot_local[None, :] == slot_ids[:, None]).astype(jnp.float32)
     term = exact_dot(gather_op, scaled)
-    total = lax.psum(term, "grp")
+    peers, total = (lax.axis_size("grp"), term)
+    for stride in [1 << k for k in range(peers.bit_length() - 1)]:
+        swap = [(i, i ^ stride) for i in range(peers)]
+        total = total + lax.ppermute(total, "grp", swap)
     spread_op = (slot_local[:, None] == slot_ids[None, :]).astype(jnp.float32)
     combined = exact_dot(spread_op, total)
     back_third = square_table(dehier_weight, P2)

time: 231 us -> 430 us (1.86)
  waiting for transfers between devices: 156 us -> 360 us
  between operations: 15 us -> 1.65 us
  starting transfers between devices: 0.01 us -> 5.82 us
    ppermute x0 -> x3, waiting for transfers between devices: none -> 360 us  [shards(): total = total + lax.ppermute(total, 'grp', swap)]
    psum x1 -> x0, waiting for transfers between devices: 156 us -> none  [shards(): total = lax.psum(term, 'grp')]
    ppermute x0 -> x3, starting transfers between devices: none -> 5.82 us  [shards(): total = total + lax.ppermute(total, 'grp', swap)]
  transfers between devices with their start and end apart: 1 -> 3, of which waited for: 1 -> 3; matrix products, arithmetic and copies ran while one was open for 1% -> 0% of each run, Pallas kernels for 0% -> 0%
where the time goes in v1:
time: 430 us; the launch traced here: 429 us
  waiting for transfers between devices  360 us (84%)
  matrix products  34.7 us (8%)
  blocking collectives  15.6 us (4%)
  local copies, waits for them, and re-layouts  6.43 us (1%)
  starting transfers between devices  5.82 us (1%)
  other arithmetic  5.15 us (1%)
    ppermute x3, waiting for transfers between devices, shards(): total = total + lax.ppermute(total, 'grp', swap)  360 us
    dot_general x8, matrix products, exact_dot(): jnp.dot(left, right, precision=lax.Precision.HIGHEST, preferred_element_t...  20.4 us
    all_gather x1, blocking collectives, shards(): planes = lax.all_gather(plane[None], 'slab', axis=0, tiled=True)  8.83 us
  transfers between devices with their start and end apart: 3, of which 3 were waited for; matrix products, arithmetic and copies ran while one was open for 0% of the time, Pallas kernels for 0%

profile of v1, /device:TPU:0, one launch (start us, length us, event | category | flops | bytes accessed | tf_op | source)
XLA Modules:
  0.0 429.4 jit_solution(9592752023994268698)
XLA Ops:
  0.8 0.1 and_select_fusion.1
  0.9 2.3 copy.16
  3.3 1.9 fusion.115
  5.2 1.5 broadcast_multiply_fusion.1
  6.7 2.4 reshape.448
  9.2 3.2 fusion.9
  12.4 2.0 fusion.40
  14.4 8.8 %all-gather = f32[32,4096]{1,0:T(8,128)S(1)} all-gather(f32[8,4096]{1,0:T(8,128)S(1)} %slice.8), channel_id=2, replica_groups=mesh['grp'=8,'slab'=4] {'slab'}, dimensions={0}, use_global_device_ids=true | all-gather | bytes 655360 | tf_op jit(solution)/shard_map/all_gather | solution.py:66
  23.3 1.2 fusion.13
  25.3 2.1 fusion.1
  27.4 1.9 fusion.30
  29.3 1.6 collective-permute-start
  30.9 91.3 %collective-permute-done = f32[256,4096]{1,0:T(8,128)S(1)} collective-permute-done((f32[256,4096]{1,0:T(8,128)S(1)}, f32[256,4096]{1,0:T(8,128)S(1)}, u32[]{:S(2)}, u32[]{:S(2)}) %collective-permute-start) | collective-permute-done | bytes 4194336 | tf_op jit(solution)/shard_map/ppermute | solution.py:93
  122.2 0.6 add.145
  122.9 1.6 collective-permute-start.1
  124.5 90.4 %collective-permute-done.1 = f32[256,4096]{1,0:T(8,128)S(1)} collective-permute-done((f32[256,4096]{1,0:T(8,128)S(1)}, f32[256,4096]{1,0:T(8,128)S(1)}, u32[]{:S(2)}, u32[]{:S(2)}) %collective-permute-start.1) | collective-permute-done | bytes 4194336 | tf_op jit(solution)/shard_map/ppermute | solution.py:93
  214.9 2.5 add.146
  217.4 2.6 collective-permute-start.2
  220.0 0.2 broadcast_multiply_fusion
  220.2 0.9 reshape.452
  221.2 178.4 %collective-permute-done.2 = f32[256,4096]{1,0:T(8,128)} collective-permute-done((f32[256,4096]{1,0:T(8,128)}, f32[256,4096]{1,0:T(8,128)}, u32[]{:S(2)}, u32[]{:S(2)}) %collective-permute-start.2) | collective-permute-done | bytes 4194336 | tf_op jit(solution)/shard_map/ppermute | solution.py:93
  399.6 5.3 %fusion.2 = f32[128,4096]{1,0:T(8,128)S(1)} fusion(f32[256,4096]{1,0:T(8,128)} %add.146, f32[256,4096]{1,0:T(8,128)} %collective-permute-done.2, s32[128]{0:T(128)S(1)} %and_select_fusion.3), kind=kOutput, calls=%fused_computation.5 | convolution fusion | flops 1611694080 | bytes 10486272 | tf_op jit(solution)/shard_map/dot_general | solution.py:43
  404.9 0.7 copy.17
  405.6 2.2 fusion.113
  407.7 3.2 fusion.7
  411.0 2.0 fusion.39
  413.0 6.8 %all-gather.1 = f32[32,4096]{1,0:T(8,128)S(1)} all-gather(f32[8,4096]{1,0:T(8,128)S(1)} %slice.9), channel_id=3, replica_groups=mesh['grp'=8,'slab'=4] {'slab'}, dimensions={0}, use_global_device_ids=true | all-gather | bytes 655360 | tf_op jit(solution)/shard_map/all_gather | solution.py:102
  419.8 1.3 fusion.17
  421.1 1.3 fusion.15
  422.3 2.0 fusion.36
  424.3 1.9 convolution_add_fusion.1
  426.2 3.2 fusion
  (25 shorter events, 0.3 us)
Async XLA Ops:
  14.4 10.9 %copy-start = (s32[1,128]{1,0:T(1,128)S(1)}, s32[1,128]{1,0:T(1,128)}, u32[]{:S(2)}) copy-start(s32[1,128]{1,0:T(1,128)} %param.7) | copy-start | bytes 1540
  29.3 92.9 %collective-permute-start = (f32[256,4096]{1,0:T(8,128)S(1)}, f32[256,4096]{1,0:T(8,128)S(1)}, u32[]{:S(2)}, u32[]{:S(2)}) collective-permute-start(f32[256,4096]{1,0:T(8,128)S(1)} %fusion.30), channel_id=1, source_target_pairs={{0,4},{4,0},{8,12},{12,8},{16,20},{20,16},{24,28},{28,24},{1,5},{5... | collective-permute-start | bytes 12582920 | tf_op jit(solution)/shard_map/ppermute | solution.py:93
  122.9 92.0 %collective-permute-start.1 = (f32[256,4096]{1,0:T(8,128)S(1)}, f32[256,4096]{1,0:T(8,128)S(1)}, u32[]{:S(2)}, u32[]{:S(2)}) collective-permute-start(f32[256,4096]{1,0:T(8,128)S(1)} %add.145), channel_id=1, source_target_pairs={{0,8},{4,12},{8,0},{12,4},{16,24},{20,28},{24,16},{28,20},{1,9},{5... | collective-permute-start | bytes 12582920 | tf_op jit(solution)/shard_map/ppermute | solution.py:93
  217.4 182.2 %collective-permute-start.2 = (f32[256,4096]{1,0:T(8,128)}, f32[256,4096]{1,0:T(8,128)}, u32[]{:S(2)}, u32[]{:S(2)}) collective-permute-start(f32[256,4096]{1,0:T(8,128)} %add.146), channel_id=1, source_target_pairs={{0,16},{4,20},{8,24},{12,28},{16,0},{20,4},{24,8},{28,12},{1,17},{... | collective-permute-start | bytes 12582920 | tf_op jit(solution)/shard_map/ppermute | solution.py:93
